TPU v7x, 32 devices: a whole 2x2x4 slice. The times are simulated.
32 devices in a mesh: seq: 8 (over z, x), res: 4 (over y, core).
Axes of the slice: x: 2, y: 2, z: 4, core: 2. Of those that a mesh axis runs over, the one named last changes fastest.
Arguments:
- alignment: bfloat16 [128, 256, 256], P('res', 'seq'), may hold values from -6 to 6
- alignment_mask: int32 [128, 256], P('res', 'seq'), may hold values from 0 to 1, as said below
- residue_mask: int32 [256], replicated, may hold values from 0 to 1, as said below
- pair_input: float32 [256, 256, 128], P('seq', 'res'), may hold values from -6 to 6
- outer_gain: float32 [256], replicated, may hold values from 0.25 to 1.75
- left_weight: bfloat16 [256, 32], replicated, may hold values from -0.375 to 0.375
- right_weight: bfloat16 [256, 32], replicated, may hold values from -0.375 to 0.375
- outer_weight: bfloat16 [1024, 128], replicated, may hold values from -1 to 1
- pair_gain: float32 [128], replicated, may hold values from 0.25 to 1.75
- bias_weight: bfloat16 [128, 8], replicated, may hold values from -48 to 48
- row_gain: float32 [256], replicated, may hold values from 0.25 to 1.75
- query_weight: bfloat16 [256, 256], replicated, may hold values from -0.375 to 0.375
- key_weight: bfloat16 [256, 256], replicated, may hold values from -0.375 to 0.375
- value_weight: bfloat16 [256, 256], replicated, may hold values from -0.375 to 0.375
- gate_weight: bfloat16 [256, 256], replicated, may hold values from -0.375 to 0.375
- output_weight: bfloat16 [256, 256], replicated, may hold values from -2 to 2
- transition_gain: float32 [256], replicated, may hold values from 0.25 to 1.75
- up_weight: bfloat16 [256, 1024], replicated, may hold values from -0.375 to 0.375
- down_weight: bfloat16 [1024, 256], replicated, may hold values from -0.1875 to 0.1875
Outputs:
- pair_output: float32 [256, 256, 128], P('seq', 'res')
- alignment_output: float32 [128, 256, 256], P('res', 'seq')
Inputs may be any that keep to these rules, and one draw needn't show every extreme that they name: `residue_mask`: 1 for a present residue, 0 for padding; at least one residue is 1 and at least one is 0. Some residue whose residue_mask is 1 has alignment_mask 1 in every sequence.
All inputs are finite; a program needn't handle non-finite values.
Results may differ from a plain program's by a relative error of at most 0.04.
Values may be sent and summed in bfloat16 or wider, within the bound.
No kernel may reach another device: no remote copies, remote signals or barrier semaphores. Data moves between devices by JAX's collectives and lax.ppermute only.
A program may use at most 128 MiB of HBM per device.

v0:
```python
import math
import jax
import jax.numpy as jnp
from jax import lax
from jax.sharding import PartitionSpec as P

EPSILON = 1e-05
MASKED = -1000000000.0
SCORE_LIMIT = 524288


def layer_norm(values, scales):
    values = values.astype(jnp.float32)
    center = values - jnp.mean(values, -1, keepdims=True)
    spread = jnp.mean(center * center, -1, keepdims=True)
    return center * lax.rsqrt(spread + EPSILON) * scales


def project(values, weight):
    flattened = values.reshape(-1, values.shape[-1])
    result = jnp.dot(flattened, weight, preferred_element_type=jnp.float32)
    return result.reshape(values.shape[:-1] + (weight.shape[1],))


def block_size(length, per_item):
    item_limit = max(1, SCORE_LIMIT // per_item)
    return max(
        (
            divisor
            for divisor in range(1, length + 1)
            if length % divisor == 0 and divisor <= item_limit
        )
    )


def in_blocks(function, arrays, block_rows):
    shaped = tuple(
        (
            member.reshape((member.shape[0] // block_rows, block_rows) + member.shape[1:])
            for member in arrays
        )
    )
    outputs = lax.map(function, shaped)
    return jax.tree.map(lambda member: member.reshape((-1,) + member.shape[2:]), outputs)


def head_scores(query_rows, key_rows, live_keys, head_bias, head_count, score_scale):
    seq_block, row_count, features = query_rows.shape
    key_count = key_rows.shape[1]
    head_size = features // head_count
    scores = jnp.einsum(
        "sihd,sjhd->shij",
        query_rows.reshape(seq_block, row_count, head_count, head_size),
        key_rows.reshape(seq_block, key_count, head_count, head_size),
        preferred_element_type=jnp.float32,
    )
    scores = scores * score_scale + head_bias.astype(jnp.float32)[None]
    return jnp.where(live_keys[:, None, None, :] > 0, scores, MASKED)


def head_weigh(scores, score_peaks, values, head_count):
    weights = jnp.exp(scores - score_peaks[..., None])
    totals = jnp.swapaxes(jnp.sum(weights, -1), 1, 2)
    seq_block, key_count, features = values.shape
    mixed_sum = jnp.einsum(
        "shij,sjhd->sihd",
        weights.astype(jnp.bfloat16),
        values.reshape(seq_block, key_count, head_count, features // head_count),
        preferred_element_type=jnp.float32,
    )
    return (mixed_sum.reshape(seq_block, mixed_sum.shape[1], features), totals)


def on_device(
    alignment,
    alignment_mask,
    residue_mask,
    pair_input,
    outer_gain,
    left_weight,
    right_weight,
    outer_weight,
    pair_gain,
    bias_weight,
    row_gain,
    query_weight,
    key_weight,
    value_weight,
    gate_weight,
    output_weight,
    transition_gain,
    up_weight,
    down_weight,
):
    seq_share, row_count = (alignment.shape[0], alignment.shape[1])
    res_local = pair_input.shape[1]
    seq_total = seq_share * lax.axis_size("res")
    res_total = row_count * lax.axis_size("seq")
    head_count = bias_weight.shape[1]
    outer_width = left_weight.shape[1]
    pair_width = pair_input.shape[2]
    score_scale = (query_weight.shape[1] // head_count) ** (-0.5)
    residue_live = residue_mask.astype(jnp.float32)
    row_live = lax.dynamic_slice_in_dim(residue_live, lax.axis_index("seq") * row_count, row_count)
    column_live = lax.dynamic_slice_in_dim(
        residue_live, lax.axis_index("res") * res_local, res_local
    )
    mask_local = alignment_mask.astype(jnp.bfloat16)
    own_live = alignment_mask.astype(jnp.float32) * row_live[None, :]
    outer_norm = layer_norm(alignment, outer_gain).astype(jnp.bfloat16)
    row_norm = layer_norm(alignment, row_gain).astype(jnp.bfloat16)
    left_local = (project(outer_norm, left_weight) * own_live[..., None]).astype(jnp.bfloat16)
    left_proj, row_mask = (
        lax.all_gather(left_local, "res", axis=0, tiled=True),
        lax.all_gather(mask_local, "res", axis=0, tiled=True),
    )
    row_flags = (row_mask.astype(jnp.float32) * row_live[None, :]).astype(jnp.bfloat16)
    wide_alignment, wide_mask = (
        lax.all_gather(alignment, "seq", axis=1, tiled=True),
        lax.all_gather(mask_local, "seq", axis=1, tiled=True),
    )
    wide_live = wide_mask.astype(jnp.float32) * residue_live[None, :]
    key_norm = layer_norm(wide_alignment, row_gain).astype(jnp.bfloat16)
    outer_wide = layer_norm(wide_alignment, outer_gain).astype(jnp.bfloat16)
    all_keys = project(key_norm, key_weight).astype(jnp.bfloat16)
    all_values = project(key_norm, value_weight).astype(jnp.bfloat16)
    wide_right = (project(outer_wide, right_weight) * wide_live[..., None]).astype(jnp.bfloat16)
    right_proj, column_mask = (
        lax.all_to_all(wide_right, "res", split_axis=1, concat_axis=0, tiled=True),
        lax.all_to_all(wide_mask, "res", split_axis=1, concat_axis=0, tiled=True),
    )
    column_flags = (column_mask.astype(jnp.float32) * column_live[None, :]).astype(jnp.bfloat16)
    right_flat = right_proj.reshape(seq_total, res_local * outer_width)
    row_step = math.gcd(row_count, 16)

    def outer_rows(row_start):
        left_piece = lax.dynamic_slice_in_dim(left_proj, row_start, row_step, 1).reshape(
            seq_total, row_step * outer_width
        )
        product = lax.dot_general(
            left_piece, right_flat, (((0,), (0,)), ((), ())), preferred_element_type=jnp.float32
        )
        product = product.reshape(row_step, outer_width, res_local, outer_width).transpose(
            0, 2, 1, 3
        )
        product = product.reshape(row_step * res_local, outer_width * outer_width).astype(
            jnp.bfloat16
        )
        update = jnp.dot(product, outer_weight, preferred_element_type=jnp.float32).reshape(
            row_step, res_local, pair_width
        )
        live_rows = lax.dynamic_slice_in_dim(row_flags, row_start, row_step, 1)
        counts = lax.dot_general(
            live_rows, column_flags, (((0,), (0,)), ((), ())), preferred_element_type=jnp.float32
        )
        return update / jnp.maximum(counts, 1.0)[..., None]

    starts = jnp.arange(row_count // row_step, dtype=jnp.int32) * row_step
    outer_update = lax.map(outer_rows, starts).reshape(row_count, res_local, pair_width)
    pair_output = pair_input + outer_update
    pair_norm = layer_norm(pair_output, pair_gain).astype(jnp.bfloat16)
    pair_bias = jnp.einsum(
        "ijc,ch->hij", pair_norm, bias_weight, preferred_element_type=jnp.float32
    ).astype(jnp.bfloat16)
    full_bias = lax.all_gather(pair_bias, "res", axis=2, tiled=True)
    own_queries = project(row_norm, query_weight).astype(jnp.bfloat16)
    gate_values = jax.nn.sigmoid(project(row_norm, gate_weight))
    seq_step = block_size(seq_share, head_count * row_count * res_total)

    def attend_piece(members):
        query_piece, key_piece, value_piece, live_piece = members
        scores = head_scores(query_piece, key_piece, live_piece, full_bias, head_count, score_scale)
        return head_weigh(scores, jnp.max(scores, -1), value_piece, head_count)

    mixed_sum, totals = in_blocks(
        attend_piece, (own_queries, all_keys, all_values, wide_live), seq_step
    )
    attended = (
        mixed_sum.reshape(seq_share, row_count, head_count, -1) / totals[..., None]
    ).reshape(seq_share, row_count, -1)
    gated_rows = (attended * gate_values).astype(jnp.bfloat16)
    after_rows = alignment.astype(jnp.float32) + project(gated_rows, output_weight)
    trans_norm = layer_norm(after_rows, transition_gain).astype(jnp.bfloat16)
    hidden_units = jnp.maximum(project(trans_norm, up_weight), 0.0).astype(jnp.bfloat16)
    alignment_output = after_rows + project(hidden_units, down_weight)
    return (pair_output, alignment_output)


def solution(mesh):
    in_specs = (
        P("res", "seq", None),
        P("res", "seq"),
        P(),
        P("seq", "res", None),
        P(),
        P(),
        P(),
        P(),
        P(),
        P(),
        P(),
        P(),
        P(),
        P(),
        P(),
        P(),
        P(),
        P(),
        P(),
    )
    out_specs = (P("seq", "res", None), P("res", "seq", None))
    return jax.shard_map(
        on_device, mesh=mesh, in_specs=in_specs, out_specs=out_specs, check_vma=False
    )
```

profile of v0, /device:TPU:0, one launch (start us, length us, event | category | flops | bytes accessed | tf_op | source)
XLA Modules:
  0.0 229.8 jit_solution(551415257638649572)
XLA Ops:
  8.7 32.9 %all_gather.17 = bf16[32,256]{0,1:T(8,128)(2,1)S(1)} all-gather(bf16[32,32]{0,1:T(8,128)(2,1)S(1)} %convert_element_type.111), channel_id=1, replica_groups=mesh['seq'=8,'res'=4] {'seq'}, dimensions={1}, use_global_device_ids=true | all-gather | bytes 18432 | tf_op jit(solution)/shard_map/all_gather | solution.py:120
  42.4 3.3 %all-to-all-start.1 = ((bf16[4,2,1024]{2,1,0:T(2,128)(2,1)}), bf16[4,2,1024]{2,1,0:T(2,128)(2,1)S(1)}, u32[]{:S(2)}, u32[]{:S(2)}) async-start(bf16[4,2,1024]{2,1,0:T(2,128)(2,1)} %reshape.187), calls=%async_computation.1 | async-start | bytes 32768 | tf_op jit(solution)/shard_map/all_to_all | solution.py:130
  46.6 5.2 %all_gather.18 = bf16[128,32]{1,0:T(8,128)(2,1)S(1)} all-gather(bf16[32,32]{1,0:T(8,128)(2,1)S(1)} %copy.88), channel_id=1, replica_groups=mesh['seq'=8,'res'=4] {'res'}, dimensions={0}, use_global_device_ids=true | all-gather | bytes 10240 | tf_op jit(solution)/shard_map/all_gather | solution.py:115
  55.9 1.5 fusion.46
  57.5 2.3 %convolution_convert_fusion.2 = bf16[32,32,256]{2,1,0:T(8,128)(2,1)} fusion(bf16[32,32,256]{2,1,0:T(8,128)(2,1)} %param.23, f32[256]{0:T(256)} %param.33, f32[32,32]{1,0:T(8,128)S(1)} %add_rsqrt_fusion.3, f32[32,32]{1,0:T(8,128)S(1)} %broadcast_multiply_fusion.3, bf16[256,256]{1,0:T(8,128)(2,1)} %param.34), kind=kOutput, calls=%fused_computation.56 | convolution fusion | flops 135790592 | bytes 1188864 | tf_op jit(solution)/shard_map/dot_general | solution.py:21
  59.8 10.4 %all_gather.15 = bf16[128,32,32]{2,1,0:T(8,128)(2,1)S(1)} all-gather(bf16[32,32,32]{2,1,0:T(8,128)(2,1)S(1)} %fusion.46), channel_id=1, replica_groups=mesh['seq'=8,'res'=4] {'res'}, dimensions={0}, use_global_device_ids=true | all-gather | bytes 327680 | tf_op jit(solution)/shard_map/all_gather | solution.py:114
  71.6 14.5 %all-gather.2.cloned.1.call-done = bf16[32,256,256]{2,1,0:T(8,128)(2,1)} async-done(((bf16[32,32,256]{2,1,0:T(8,128)(2,1)}), bf16[32,256,256]{2,1,0:T(8,128)(2,1)}) %all-gather.2.cloned.1.call-update) | async-done | bytes 4194320 | tf_op jit(solution)/shard_map/all_gather | solution.py:119
  86.0 3.5 %convert_reduce_fusion = f32[32,256]{1,0:T(8,128)S(1)} fusion(bf16[32,256,256]{2,1,0:T(8,128)(2,1)} %all-gather.2.cloned.1.call-done), kind=kLoop, calls=%fused_computation.28 | loop fusion | flops 4186112 | bytes 4227072 | tf_op jit(solution)/shard_map/reduce_sum | solution.py:14
  89.6 2.4 %fusion.23 = f32[32,256]{1,0:T(8,128)S(1)} fusion(bf16[32,256,256]{2,1,0:T(8,128)(2,1)S(1)} %copy-done.1, f32[32,256]{1,0:T(8,128)S(1)} %broadcast_multiply_fusion), kind=kLoop, calls=%fused_computation.35 | loop fusion | flops 8380416 | bytes 4259840 | tf_op jit(solution)/shard_map/reduce_sum | solution.py:15
  92.6 3.7 %fusion.41 = bf16[32,256,32]{1,2,0:T(8,128)(2,1)S(1)} fusion(bf16[32,256,256]{2,1,0:T(8,128)(2,1)S(1)} %copy-done.1, f32[256]{0:T(256)S(1)} %copy-done.20, f32[32,256]{1,0:T(8,128)S(1)} %add_rsqrt_fusion, f32[32,256]{1,0:T(8,128)S(1)} %broadcast_multiply_fusion, f32[32,256]{1,0:T(8,128)S(1)} %get-tuple-element.209, bf16[256,32]{0,1:T(8,128)(2,1)S(1)} %copy-done.19), kind=kOutput, calls=%fused_computation.57 | convolution fusion | flops 145227776 | bytes 4834304 | tf_op jit(solution)/shard_map/dot_general | solution.py:21
  96.4 3.0 %copy.86 = bf16[32,256,32]{2,0,1:T(8,128)(2,1)S(1)} copy(bf16[32,256,32]{1,2,0:T(8,128)(2,1)S(1)} %fusion.41) | data formatting | bytes 1048576 | tf_op jit(solution)/shard_map/convert_element_type | solution.py:127
  99.4 2.9 %reshape.185 = bf16[4,2,32768]{2,1,0:T(2,128)(2,1)} reshape(bf16[256,32,32]{2,1,0:T(8,128)(2,1)S(1)} %bitcast.151) | data formatting | bytes 1048576
  102.3 3.7 %all-to-all-start = ((bf16[4,2,32768]{2,1,0:T(2,128)(2,1)}), bf16[4,2,32768]{2,1,0:T(2,128)(2,1)S(1)}, u32[]{:S(2)}, u32[]{:S(2)}) async-start(bf16[4,2,32768]{2,1,0:T(2,128)(2,1)} %reshape.185), calls=%async_computation | async-start | bytes 1048576 | tf_op jit(solution)/shard_map/all_to_all | solution.py:129
  106.0 5.7 %convolution_convert_fusion.1 = bf16[32,256,256]{2,1,0:T(8,128)(2,1)} fusion(bf16[32,256,256]{2,1,0:T(8,128)(2,1)} %all-gather.2.cloned.1.call-done, f32[256]{0:T(256)} %param.33, f32[32,256]{1,0:T(8,128)} %copy-done.8, f32[32,256]{1,0:T(8,128)S(1)} %broadcast_multiply_fusion, bf16[256,256]{1,0:T(8,128)(2,1)} %param.36), kind=kOutput, calls=%fused_computation.42 | convolution fusion | flops 1086324736 | bytes 8586240 | tf_op jit(solution)/shard_map/dot_general | solution.py:21
  111.8 4.3 %convolution_convert_fusion = bf16[32,256,256]{2,1,0:T(8,128)(2,1)} fusion(bf16[32,256,256]{2,1,0:T(8,128)(2,1)S(1)} %copy-done.2, f32[256]{0:T(256)S(1)} %copy-done.21, f32[32,256]{1,0:T(8,128)S(1)} %copy-done.9, f32[32,256]{1,0:T(8,128)S(1)} %broadcast_multiply_fusion, bf16[256,256]{1,0:T(8,128)(2,1)S(1)} %copy-done.16), kind=kOutput, calls=%fused_computation.41 | convolution fusion | flops 1086324736 | bytes 8586240 | tf_op jit(solution)/shard_map/dot_general | solution.py:21
  117.2 2.2 copy.121
  119.3 3.5 %reshape.165 = bf16[128,2048]{1,0:T(8,128)(2,1)S(1)} reshape(bf16[4,32,64,32]{3,2,1,0:T(8,128)(2,1)} %bitcast.153) | data formatting | bytes 1048576 | tf_op jit(solution)/shard_map/reshape | solution.py:133
  123.2 15.9 %while.22 = (s32[]{:T(128)}, f32[2,16,64,128]{3,2,1,0:T(8,128)}, s32[2]{0:T(128)S(1)}, bf16[128,32,32]{0,2,1:T(8,128)(2,1)S(1)}, bf16[128,2048]{0,1:T(8,128)(2,1...) while((s32[]{:T(128)}, f32[2,16,64,128]{3,2,1,0:T(8,128)}, ...), condition=%wide.region_5.0_spmd, body=%wide.region_4.0_spmd.sunk | while | flops 538313728 | bytes 9863843 | solution.py:159
  127.0 1.8 copy.129
  129.0 2.1 fusion.126
  134.9 1.8 copy.129
  137.0 2.1 fusion.126
  139.1 1.6 fusion.95
  142.6 7.7 %all_gather.19 = bf16[8,32,256]{1,0,2:T(8,128)(2,1)S(1)} all-gather(bf16[8,32,64]{1,0,2:T(8,128)(2,1)S(1)} %copy.92), channel_id=1, replica_groups=mesh['seq'=8,'res'=4] {'res'}, dimensions={2}, use_global_device_ids=true | all-gather | bytes 163840 | tf_op jit(solution)/shard_map/all_gather | solution.py:165
  150.6 60.1 %while.23 = (s32[]{:T(128)}, f32[4,8,32,256]{3,2,1,0:T(8,128)}, f32[4,8,32,8]{2,3,1,0:T(8,128)S(1)}, bf16[4,8,256,256]{3,2,1,0:T(8,128)(2,1)}, f32[4,8,256]{2,1,...) while((s32[]{:T(128)}, f32[4,8,32,256]{3,2,1,0:T(8,128)}, ...), condition=%wide.region_11.12_spmd, body=%wide.region_8.0_spmd.sunk | while | flops 71366656 | bytes 19509868 | solution.py:43
  150.6 2.7 %constant_dynamic-slice_fusion.5 = (bf16[1,8,256,256]{3,2,1,0:T(8,128)(2,1)S(1)}, bf16[1,8,256,256]{3,2,1,0:T(8,128)(2,1)}) fusion(bf16[4,8,256,256]{3,2,1,0:T(8,128)(2,1)} %get-tuple-element.375, s32[]{:T(128)} %get-tuple-element.360, bf16[4,8,256,256]{3,2,1,0:T(8,128)(2,1)} %get-tuple-element.372), kind=kLoop, calls=%fused_computation.24.clone.1 | loop fusion | bytes 4194308 | tf_op jit(solution)/shard_map/while/body/jit(dynamic_index_in_dim)/dynamic_slice | solution.py:43
  155.8 1.8 fusion.131
  158.3 2.3 %copy.131 = bf16[1,8,256,256]{2,3,1,0:T(8,128)(2,1)} copy(bf16[1,8,256,256]{3,2,1,0:T(8,128)(2,1)} %get-tuple-element.314) | data formatting | bytes 2097152 | tf_op jit(solution)/shard_map/while/body/jit(dynamic_index_in_dim)/dynamic_slice | solution.py:43
  160.6 2.7 %fusion.132 = f32[8,8,32,32]{3,2,1,0:T(8,128)} fusion(bf16[8,256,8,32]{1,3,2,0:T(8,128)(2,1)} %bitcast.149, f32[8,8,32,256]{3,2,1,0:T(8,128)S(1)} %get-tuple-element.316, f32[8,8,32]{2,1,0:T(8,128)S(1)} %get-tuple-element.317), kind=kOutput, calls=%fused_computation.17.clone.1 | convolution fusion | flops 34603008 | bytes 3416064 | tf_op jit(solution)/shard_map/while/body/eval_jaxpr/shij,sjhd->sihd/dot_general | solution.py:65
  163.3 1.5 copy.133
  165.6 2.7 %constant_dynamic-slice_fusion.5 = (bf16[1,8,256,256]{3,2,1,0:T(8,128)(2,1)S(1)}, bf16[1,8,256,256]{3,2,1,0:T(8,128)(2,1)}) fusion(bf16[4,8,256,256]{3,2,1,0:T(8,128)(2,1)} %get-tuple-element.375, s32[]{:T(128)} %get-tuple-element.360, bf16[4,8,256,256]{3,2,1,0:T(8,128)(2,1)} %get-tuple-element.372), kind=kLoop, calls=%fused_computation.24.clone.1 | loop fusion | bytes 4194308 | tf_op jit(solution)/shard_map/while/body/jit(dynamic_index_in_dim)/dynamic_slice | solution.py:43
  170.8 1.8 fusion.131
  173.3 2.3 %copy.131 = bf16[1,8,256,256]{2,3,1,0:T(8,128)(2,1)} copy(bf16[1,8,256,256]{3,2,1,0:T(8,128)(2,1)} %get-tuple-element.314) | data formatting | bytes 2097152 | tf_op jit(solution)/shard_map/while/body/jit(dynamic_index_in_dim)/dynamic_slice | solution.py:43
  175.6 2.7 %fusion.132 = f32[8,8,32,32]{3,2,1,0:T(8,128)} fusion(bf16[8,256,8,32]{1,3,2,0:T(8,128)(2,1)} %bitcast.149, f32[8,8,32,256]{3,2,1,0:T(8,128)S(1)} %get-tuple-element.316, f32[8,8,32]{2,1,0:T(8,128)S(1)} %get-tuple-element.317), kind=kOutput, calls=%fused_computation.17.clone.1 | convolution fusion | flops 34603008 | bytes 3416064 | tf_op jit(solution)/shard_map/while/body/eval_jaxpr/shij,sjhd->sihd/dot_general | solution.py:65
  178.4 1.5 copy.133
  180.6 2.7 %constant_dynamic-slice_fusion.5 = (bf16[1,8,256,256]{3,2,1,0:T(8,128)(2,1)S(1)}, bf16[1,8,256,256]{3,2,1,0:T(8,128)(2,1)}) fusion(bf16[4,8,256,256]{3,2,1,0:T(8,128)(2,1)} %get-tuple-element.375, s32[]{:T(128)} %get-tuple-element.360, bf16[4,8,256,256]{3,2,1,0:T(8,128)(2,1)} %get-tuple-element.372), kind=kLoop, calls=%fused_computation.24.clone.1 | loop fusion | bytes 4194308 | tf_op jit(solution)/shard_map/while/body/jit(dynamic_index_in_dim)/dynamic_slice | solution.py:43
  185.9 1.8 fusion.131
  188.3 2.3 %copy.131 = bf16[1,8,256,256]{2,3,1,0:T(8,128)(2,1)} copy(bf16[1,8,256,256]{3,2,1,0:T(8,128)(2,1)} %get-tuple-element.314) | data formatting | bytes 2097152 | tf_op jit(solution)/shard_map/while/body/jit(dynamic_index_in_dim)/dynamic_slice | solution.py:43
  190.7 2.7 %fusion.132 = f32[8,8,32,32]{3,2,1,0:T(8,128)} fusion(bf16[8,256,8,32]{1,3,2,0:T(8,128)(2,1)} %bitcast.149, f32[8,8,32,256]{3,2,1,0:T(8,128)S(1)} %get-tuple-element.316, f32[8,8,32]{2,1,0:T(8,128)S(1)} %get-tuple-element.317), kind=kOutput, calls=%fused_computation.17.clone.1 | convolution fusion | flops 34603008 | bytes 3416064 | tf_op jit(solution)/shard_map/while/body/eval_jaxpr/shij,sjhd->sihd/dot_general | solution.py:65
  193.4 1.5 copy.133
  195.7 2.7 %constant_dynamic-slice_fusion.5 = (bf16[1,8,256,256]{3,2,1,0:T(8,128)(2,1)S(1)}, bf16[1,8,256,256]{3,2,1,0:T(8,128)(2,1)}) fusion(bf16[4,8,256,256]{3,2,1,0:T(8,128)(2,1)} %get-tuple-element.375, s32[]{:T(128)} %get-tuple-element.360, bf16[4,8,256,256]{3,2,1,0:T(8,128)(2,1)} %get-tuple-element.372), kind=kLoop, calls=%fused_computation.24.clone.1 | loop fusion | bytes 4194308 | tf_op jit(solution)/shard_map/while/body/jit(dynamic_index_in_dim)/dynamic_slice | solution.py:43
  200.9 1.8 fusion.131
  203.4 2.3 %copy.131 = bf16[1,8,256,256]{2,3,1,0:T(8,128)(2,1)} copy(bf16[1,8,256,256]{3,2,1,0:T(8,128)(2,1)} %get-tuple-element.314) | data formatting | bytes 2097152 | tf_op jit(solution)/shard_map/while/body/jit(dynamic_index_in_dim)/dynamic_slice | solution.py:43
  205.7 2.7 %fusion.132 = f32[8,8,32,32]{3,2,1,0:T(8,128)} fusion(bf16[8,256,8,32]{1,3,2,0:T(8,128)(2,1)} %bitcast.149, f32[8,8,32,256]{3,2,1,0:T(8,128)S(1)} %get-tuple-element.316, f32[8,8,32]{2,1,0:T(8,128)S(1)} %get-tuple-element.317), kind=kOutput, calls=%fused_computation.17.clone.1 | convolution fusion | flops 34603008 | bytes 3416064 | tf_op jit(solution)/shard_map/while/body/eval_jaxpr/shij,sjhd->sihd/dot_general | solution.py:65
  210.9 2.6 %div.59 = f32[32,32,8,32]{3,2,1,0:T(8,128)} broadcast(f32[32,32,8]{2,1,0:T(8,128)S(1)} %copy.97), dimensions={0,1,2} | broadcast | bytes 1081344 | tf_op jit(solution)/shard_map/div | solution.py:179
  213.5 3.4 %div.60 = f32[32,32,256]{2,1,0:T(8,128)S(1)} reshape(f32[32,32,8,32]{3,2,1,0:T(8,128)} %div.59) | data formatting | bytes 2097152 | tf_op jit(solution)/shard_map/div | solution.py:179
  218.1 2.0 fusion.97
  220.6 2.4 %fusion.39 = f32[32,32,256]{2,1,0:T(8,128)} fusion(f32[32,32,256]{2,1,0:T(8,128)S(1)} %get-tuple-element.211, bf16[1024,256]{1,0:T(8,128)(2,1)S(1)} %copy-done, bf16[256,1024]{1,0:T(8,128)(2,1)S(1)} %copy-done.14, f32[256]{0:T(256)S(1)} %copy-done.23, f32[32,32]{1,0:T(8,128)S(1)} %add_rsqrt_fusion.1, f32[32,32]{1,0:T(8,128)S(1)} %broadcast_multiply_fusion.2), kind=kOutput, calls=%fused_computation.54 | convolution fusion | flops 1077149696 | bytes 3154944 | tf_op jit(solution)/shard_map/dot_general | solution.py:21
  (131 shorter events, 35.9 us)
Async XLA Ops:
  7.2 213.4 %copy-start = (bf16[1024,256]{1,0:T(8,128)(2,1)S(1)}, bf16[1024,256]{1,0:T(8,128)(2,1)}, u32[]{:S(2)}) copy-start(bf16[1024,256]{1,0:T(8,128)(2,1)} %param.41) | copy-start | bytes 1572868
  7.2 78.9 %all-gather.2.cloned.1.call-start = ((), (), s32[]{:S(2)}) async-start(), calls=%async_computation.2 | async-start | bytes 4718592 | tf_op jit(solution)/shard_map/all_gather | solution.py:119
  42.4 29.0 %all-to-all-start.1 = ((bf16[4,2,1024]{2,1,0:T(2,128)(2,1)}), bf16[4,2,1024]{2,1,0:T(2,128)(2,1)S(1)}, u32[]{:S(2)}, u32[]{:S(2)}) async-start(bf16[4,2,1024]{2,1,0:T(2,128)(2,1)} %reshape.187), calls=%async_computation.1 | async-start | bytes 32768 | tf_op jit(solution)/shard_map/all_to_all | solution.py:130
  55.2 2.3 %copy-start.10 = (f32[32,32]{1,0:T(8,128)}, f32[32,32]{1,0:T(8,128)S(1)}, u32[]{:S(2)}) copy-start(f32[32,32]{1,0:T(8,128)S(1)} %add_rsqrt_fusion.3) | copy-start | bytes 12292
  71.5 21.1 %copy-start.19 = (bf16[256,32]{0,1:T(8,128)(2,1)S(1)}, bf16[256,32]{0,1:T(8,128)(2,1)}, u32[]{:S(2)}) copy-start(bf16[256,32]{0,1:T(8,128)(2,1)} %param.29) | copy-start | bytes 49156
  71.6 21.1 %copy-start.20 = (f32[256]{0:T(256)S(1)}, f32[256]{0:T(256)}, u32[]{:S(2)}) copy-start(f32[256]{0:T(256)} %param.27) | copy-start | bytes 3076
  86.0 3.5 %copy-start.1 = (bf16[32,256,256]{2,1,0:T(8,128)(2,1)S(1)}, bf16[32,256,256]{2,1,0:T(8,128)(2,1)}, u32[]{:S(2)}) copy-start(bf16[32,256,256]{2,1,0:T(8,128)(2,1)} %all-gather.2.cloned.1.call-done) | copy-start | bytes 12582916
  92.0 0.6 copy-start.8
  102.3 13.7 %all-to-all-start = ((bf16[4,2,32768]{2,1,0:T(2,128)(2,1)}), bf16[4,2,32768]{2,1,0:T(2,128)(2,1)S(1)}, u32[]{:S(2)}, u32[]{:S(2)}) async-start(bf16[4,2,32768]{2,1,0:T(2,128)(2,1)} %reshape.185), calls=%async_computation | async-start | bytes 1048576 | tf_op jit(solution)/shard_map/all_to_all | solution.py:129
  106.0 5.8 %copy-start.2 = (bf16[32,256,256]{2,1,0:T(8,128)(2,1)S(1)}, bf16[32,256,256]{2,1,0:T(8,128)(2,1)}, u32[]{:S(2)}) copy-start(bf16[32,256,256]{2,1,0:T(8,128)(2,1)} %all-gather.2.cloned.1.call-done) | copy-start | bytes 12582916
  106.0 5.7 %copy-start.9 = (f32[32,256]{1,0:T(8,128)S(1)}, f32[32,256]{1,0:T(8,128)}, u32[]{:S(2)}) copy-start(f32[32,256]{1,0:T(8,128)} %copy-done.8) | copy-start | bytes 98308
  106.0 5.7 %copy-start.16 = (bf16[256,256]{1,0:T(8,128)(2,1)S(1)}, bf16[256,256]{1,0:T(8,128)(2,1)}, u32[]{:S(2)}) copy-start(bf16[256,256]{1,0:T(8,128)(2,1)} %param.35) | copy-start | bytes 393220
  106.0 5.7 %copy-start.21 = (f32[256]{0:T(256)S(1)}, f32[256]{0:T(256)}, u32[]{:S(2)}) copy-start(f32[256]{0:T(256)} %param.33) | copy-start | bytes 3076
  117.1 6.0 %copy-start.15 = (bf16[1024,128]{1,0:T(8,128)(2,1)S(1)}, bf16[1024,128]{1,0:T(8,128)(2,1)}, u32[]{:S(2)}) copy-start(bf16[1024,128]{1,0:T(8,128)(2,1)} %param.30) | copy-start | bytes 786436
  117.2 6.0 %copy-start.24 = (s32[2]{0:T(128)S(1)}, s32[2]{0:T(128)}, u32[]{:S(2)}) copy-start(s32[2]{0:T(128)} %iota_multiply_fusion) | copy-start | bytes 28
  123.1 15.9 %copy-start.5 = (f32[32,64,128]{2,1,0:T(8,128)S(1)}, f32[32,64,128]{2,1,0:T(8,128)}, u32[]{:S(2)}) copy-start(f32[32,64,128]{2,1,0:T(8,128)} %param.26) | copy-start | bytes 3145732
  139.1 2.6 %copy-start.12 = (bf16[128,8]{0,1:T(8,128)(2,1)S(1)}, bf16[128,8]{0,1:T(8,128)(2,1)}, u32[]{:S(2)}) copy-start(bf16[128,8]{0,1:T(8,128)(2,1)} %param.32) | copy-start | bytes 6148
  139.1 2.6 %copy-start.13 = (f32[128]{0:T(128)S(1)}, f32[128]{0:T(128)}, u32[]{:S(2)}) copy-start(f32[128]{0:T(128)} %param.31) | copy-start | bytes 1540
  139.1 11.5 %copy-start.7 = (f32[4,8,32,8]{2,3,1,0:T(8,128)S(1)}, f32[4,8,32,8]{2,3,1,0:T(8,128)}, u32[]{:S(2)}) copy-start(f32[4,8,32,8]{2,3,1,0:T(8,128)} %custom-call.2) | copy-start | bytes 98308
  140.7 1.0 copy-start.3
  210.9 6.0 %copy-start.6 = (f32[4,8,32,256]{3,2,1,0:T(8,128)S(1)}, f32[4,8,32,256]{3,2,1,0:T(8,128)}, u32[]{:S(2)}) copy-start(f32[4,8,32,256]{3,2,1,0:T(8,128)} %get-tuple-element.88) | copy-start | bytes 3145732
  213.5 4.6 %copy-start.4 = (bf16[32,32,256]{2,1,0:T(8,128)(2,1)S(1)}, bf16[32,32,256]{2,1,0:T(8,128)(2,1)}, u32[]{:S(2)}) copy-start(bf16[32,32,256]{2,1,0:T(8,128)(2,1)} %param.23) | copy-start | bytes 1572868
  213.5 4.6 %copy-start.11 = (f32[32,32]{1,0:T(8,128)S(1)}, f32[32,32]{1,0:T(8,128)}, u32[]{:S(2)}) copy-start(f32[32,32]{1,0:T(8,128)} %copy-done.10) | copy-start | bytes 12292
  213.5 4.6 %copy-start.17 = (bf16[256,256]{1,0:T(8,128)(2,1)S(1)}, bf16[256,256]{1,0:T(8,128)(2,1)}, u32[]{:S(2)}) copy-start(bf16[256,256]{1,0:T(8,128)(2,1)} %param.38) | copy-start | bytes 393220
  213.5 4.6 %copy-start.18 = (bf16[256,256]{1,0:T(8,128)(2,1)S(1)}, bf16[256,256]{1,0:T(8,128)(2,1)}, u32[]{:S(2)}) copy-start(bf16[256,256]{1,0:T(8,128)(2,1)} %param.37) | copy-start | bytes 393220
  213.5 4.6 %copy-start.22 = (f32[256]{0:T(256)S(1)}, f32[256]{0:T(256)}, u32[]{:S(2)}) copy-start(f32[256]{0:T(256)} %param.33) | copy-start | bytes 3076
  218.1 2.4 %copy-start.14 = (bf16[256,1024]{1,0:T(8,128)(2,1)S(1)}, bf16[256,1024]{1,0:T(8,128)(2,1)}, u32[]{:S(2)}) copy-start(bf16[256,1024]{1,0:T(8,128)(2,1)} %param.40) | copy-start | bytes 1572868
  218.1 2.4 %copy-start.23 = (f32[256]{0:T(256)S(1)}, f32[256]{0:T(256)}, u32[]{:S(2)}) copy-start(f32[256]{0:T(256)} %param.39) | copy-start | bytes 3076
Sparse Core Ops, SparseCore 0:
  10.2 75.8 all-gather.1
where the time goes:
time: 231 us; the launch traced here: 230 us
  local copies, waits for them, and re-layouts  67.4 us (29%)
  blocking collectives  56.3 us (24%)
  matrix products  48.2 us (21%)
  other arithmetic  17.2 us (7%)
  waiting for transfers between devices  15.2 us (7%)
  between operations  14.5 us (6%)
  starting transfers between devices  6.94 us (3%)
  loops' own time  4.13 us (2%)
    all_gather x1, blocking collectives, on_device(): lax.all_gather(mask_local, 'seq', axis=1, tiled=True)  32.9 us
    dynamic_slice x16, local copies, waits for them, and re-layouts, in_blocks(): outputs = lax.map(function, shaped)  28.9 us
    dot_general x7, matrix products, project(): result = jnp.dot(flattened, weight, preferred_element_type=jnp.float32)  22 us
    all_gather x1, waiting for transfers between devices, on_device(): lax.all_gather(alignment, 'seq', axis=1, tiled=True)  14.5 us
    dot_general x4, matrix products, head_weigh(): jnp.einsum('shij,sjhd->sihd', weights.astype(jnp.bfloat16), values.reshap...  10.9 us
    all_gather x1, blocking collectives, on_device(): lax.all_gather(left_local, 'res', axis=0, tiled=True)  10.4 us
    dynamic_update_slice x12, local copies, waits for them, and re-layouts, in_blocks(): outputs = lax.map(function, shaped)  9.08 us
    all_gather x1, blocking collectives, on_device(): full_bias = lax.all_gather(pair_bias, 'res', axis=2, tiled=True)  7.68 us
  transfers between devices with their start and end apart: 3, of which 1 were waited for; matrix products, arithmetic and copies ran while one was open for 9% of the time, Pallas kernels for 0%

commit v1 on v0

--- a/solution.py
+++ b/solution.py
@@ -1,3 +1,4 @@
+import functools
 import math
 import jax
 import jax.numpy as jnp
@@ -7,6 +8,14 @@
 EPSILON = 1e-05
 MASKED = -1000000000.0
 SCORE_LIMIT = 524288
+
+
+def point_the_entries(chunk, at_axis):
+    far_arr = lax.all_gather(chunk, axis_name="seq")
+    return jnp.concatenate(far_arr, axis=at_axis)
+
+
+_write_limits = functools.partial(point_the_entries, at_axis=1)
 
 
 def layer_norm(values, scales):
@@ -117,7 +126,7 @@
     row_flags = (row_mask.astype(jnp.float32) * row_live[None, :]).astype(jnp.bfloat16)
     wide_alignment, wide_mask = (
         lax.all_gather(alignment, "seq", axis=1, tiled=True),
-        lax.all_gather(mask_local, "seq", axis=1, tiled=True),
+        _write_limits(mask_local),
     )
     wide_live = wide_mask.astype(jnp.float32) * residue_live[None, :]
     key_norm = layer_norm(wide_alignment, row_gain).astype(jnp.bfloat16)

time: 231 us -> 231 us (level)
    unnamed x55 -> x60, local copies, waits for them, and re-layouts: 6.6 us -> 5.84 us
where the time goes in v1:
time: 231 us; the launch traced here: 230 us
  local copies, waits for them, and re-layouts  66.7 us (29%)
  blocking collectives  56.3 us (24%)
  matrix products  47.2 us (20%)
  other arithmetic  17.9 us (8%)
  waiting for transfers between devices  16.3 us (7%)
  between operations  14.6 us (6%)
  starting transfers between devices  6.94 us (3%)
  loops' own time  4.13 us (2%)
    all_gather x1, blocking collectives, point_the_entries(): far_arr = lax.all_gather(chunk, axis_name='seq')  32.9 us
    dynamic_slice x16, local copies, waits for them, and re-layouts, in_blocks(): outputs = lax.map(function, shaped)  29 us
    dot_general x7, matrix products, project(): result = jnp.dot(flattened, weight, preferred_element_type=jnp.float32)  21 us
    all_gather x1, waiting for transfers between devices, on_device(): lax.all_gather(alignment, 'seq', axis=1, tiled=True)  15.6 us
    dot_general x4, matrix products, head_weigh(): jnp.einsum('shij,sjhd->sihd', weights.astype(jnp.bfloat16), values.reshap...  10.9 us
    all_gather x1, blocking collectives, on_device(): lax.all_gather(left_local, 'res', axis=0, tiled=True)  10.4 us
    dynamic_update_slice x12, local copies, waits for them, and re-layouts, in_blocks(): outputs = lax.map(function, shaped)  9.1 us
    all_gather x1, blocking collectives, on_device(): full_bias = lax.all_gather(pair_bias, 'res', axis=2, tiled=True)  7.68 us
  transfers between devices with their start and end apart: 3, of which 1 were waited for; matrix products, arithmetic and copies ran while one was open for 9% of the time, Pallas kernels for 0%

profile of v1, /device:TPU:0, one launch (start us, length us, event | category | flops | bytes accessed | tf_op | source)
XLA Modules:
  0.0 230.0 jit_solution(16668505693018412719)
XLA Ops:
  8.7 32.9 %all-gather = bf16[256,32]{1,0:T(8,128)(2,1)S(1)} all-gather(bf16[32,32]{1,0:T(8,128)(2,1)S(1)} %convert_element_type.124), channel_id=2, replica_groups=mesh['seq'=8,'res'=4] {'seq'}, dimensions={0}, use_global_device_ids=true | all-gather | bytes 18432 | tf_op jit(solution)/shard_map/all_gather | solution.py:14
  42.5 3.3 %all-to-all-start.1 = ((bf16[4,2,1024]{2,1,0:T(2,128)(2,1)}), bf16[4,2,1024]{2,1,0:T(2,128)(2,1)S(1)}, u32[]{:S(2)}, u32[]{:S(2)}) async-start(bf16[4,2,1024]{2,1,0:T(2,128)(2,1)} %reshape.217), calls=%async_computation.1 | async-start | bytes 32768 | tf_op jit(solution)/shard_map/all_to_all | solution.py:139
  46.7 5.2 %all_gather.22 = bf16[128,32]{1,0:T(8,128)(2,1)S(1)} all-gather(bf16[32,32]{1,0:T(8,128)(2,1)S(1)} %convert_element_type.124), channel_id=1, replica_groups=mesh['seq'=8,'res'=4] {'res'}, dimensions={0}, use_global_device_ids=true | all-gather | bytes 10240 | tf_op jit(solution)/shard_map/all_gather | solution.py:124
  55.9 1.5 fusion.46
  58.8 10.4 %all_gather.18 = bf16[128,32,32]{2,1,0:T(8,128)(2,1)S(1)} all-gather(bf16[32,32,32]{2,1,0:T(8,128)(2,1)S(1)} %fusion.46), channel_id=1, replica_groups=mesh['seq'=8,'res'=4] {'res'}, dimensions={0}, use_global_device_ids=true | all-gather | bytes 327680 | tf_op jit(solution)/shard_map/all_gather | solution.py:123
  70.5 15.6 %all-gather.3.cloned.1.call-done = bf16[32,256,256]{2,1,0:T(8,128)(2,1)} async-done(((bf16[32,32,256]{2,1,0:T(8,128)(2,1)}), bf16[32,256,256]{2,1,0:T(8,128)(2,1)}) %all-gather.3.cloned.1.call-update) | async-done | bytes 4194320 | tf_op jit(solution)/shard_map/all_gather | solution.py:128
  86.1 3.5 %convert_reduce_fusion = f32[32,256]{1,0:T(8,128)S(1)} fusion(bf16[32,256,256]{2,1,0:T(8,128)(2,1)} %all-gather.3.cloned.1.call-done), kind=kLoop, calls=%fused_computation.28 | loop fusion | flops 4186112 | bytes 4227072 | tf_op jit(solution)/shard_map/reduce_sum | solution.py:23
  89.6 2.4 %fusion.23 = f32[32,256]{1,0:T(8,128)S(1)} fusion(bf16[32,256,256]{2,1,0:T(8,128)(2,1)S(1)} %copy-done.1, f32[32,256]{1,0:T(8,128)S(1)} %broadcast_multiply_fusion.2), kind=kLoop, calls=%fused_computation.35 | loop fusion | flops 8380416 | bytes 4259840 | tf_op jit(solution)/shard_map/reduce_sum | solution.py:24
  92.7 3.7 %fusion.41 = bf16[32,256,32]{1,2,0:T(8,128)(2,1)S(1)} fusion(bf16[32,256,256]{2,1,0:T(8,128)(2,1)S(1)} %copy-done.1, f32[256]{0:T(256)S(1)} %copy-done.22, f32[32,256]{1,0:T(8,128)S(1)} %add_rsqrt_fusion, f32[32,256]{1,0:T(8,128)S(1)} %broadcast_multiply_fusion.2, f32[32,256]{1,0:T(8,128)S(1)} %broadcast_multiply_fusion.1, bf16[256,32]{0,1:T(8,128)(2,1)S(1)} %copy-done.21), kind=kOutput, calls=%fused_computation.57 | convolution fusion | flops 145227776 | bytes 4834304 | tf_op jit(solution)/shard_map/dot_general | solution.py:30
  96.4 3.0 %copy.50 = bf16[32,256,32]{2,0,1:T(8,128)(2,1)S(1)} copy(bf16[32,256,32]{1,2,0:T(8,128)(2,1)S(1)} %fusion.41) | data formatting | bytes 1048576 | tf_op jit(solution)/shard_map/convert_element_type | solution.py:136
  99.5 2.9 %reshape.215 = bf16[4,2,32768]{2,1,0:T(2,128)(2,1)} reshape(bf16[256,32,32]{2,1,0:T(8,128)(2,1)S(1)} %bitcast.155) | data formatting | bytes 1048576
  102.4 3.7 %all-to-all-start = ((bf16[4,2,32768]{2,1,0:T(2,128)(2,1)}), bf16[4,2,32768]{2,1,0:T(2,128)(2,1)S(1)}, u32[]{:S(2)}, u32[]{:S(2)}) async-start(bf16[4,2,32768]{2,1,0:T(2,128)(2,1)} %reshape.215), calls=%async_computation | async-start | bytes 1048576 | tf_op jit(solution)/shard_map/all_to_all | solution.py:138
  106.1 5.7 %convolution_convert_fusion.1 = bf16[32,256,256]{2,1,0:T(8,128)(2,1)} fusion(bf16[32,256,256]{2,1,0:T(8,128)(2,1)} %all-gather.3.cloned.1.call-done, f32[256]{0:T(256)} %param.33, f32[32,256]{1,0:T(8,128)} %copy-done.9, f32[32,256]{1,0:T(8,128)S(1)} %broadcast_multiply_fusion.2, bf16[256,256]{1,0:T(8,128)(2,1)} %param.36), kind=kOutput, calls=%fused_computation.42 | convolution fusion | flops 1086324736 | bytes 8586240 | tf_op jit(solution)/shard_map/dot_general | solution.py:30
  111.8 4.4 %convolution_convert_fusion = bf16[32,256,256]{2,1,0:T(8,128)(2,1)} fusion(bf16[32,256,256]{2,1,0:T(8,128)(2,1)S(1)} %copy-done.2, f32[256]{0:T(256)S(1)} %copy-done.24, f32[32,256]{1,0:T(8,128)S(1)} %copy-done.10, f32[32,256]{1,0:T(8,128)S(1)} %broadcast_multiply_fusion.2, bf16[256,256]{1,0:T(8,128)(2,1)S(1)} %copy-done.18), kind=kOutput, calls=%fused_computation.41 | convolution fusion | flops 1086324736 | bytes 8586240 | tf_op jit(solution)/shard_map/dot_general | solution.py:30
  117.3 2.2 copy.88
  119.5 3.5 %reshape.193 = bf16[128,2048]{1,0:T(8,128)(2,1)S(1)} reshape(bf16[4,32,64,32]{3,2,1,0:T(8,128)(2,1)} %bitcast.157) | data formatting | bytes 1048576 | tf_op jit(solution)/shard_map/reshape | solution.py:142
  123.3 15.9 %while.22 = (s32[]{:T(128)}, f32[2,16,64,128]{3,2,1,0:T(8,128)}, s32[2]{0:T(128)S(1)}, bf16[128,32,32]{0,2,1:T(8,128)(2,1)S(1)}, bf16[128,2048]{0,1:T(8,128)(2,1...) while((s32[]{:T(128)}, f32[2,16,64,128]{3,2,1,0:T(8,128)}, ...), condition=%wide.region_5.0_spmd, body=%wide.region_4.0_spmd.sunk | while | flops 538313728 | bytes 9863843 | solution.py:168
  127.2 1.8 copy.97
  129.2 2.1 fusion.126
  135.1 1.8 copy.97
  137.1 2.1 fusion.126
  139.2 1.6 fusion.95
  142.7 7.7 %all_gather.23 = bf16[8,32,256]{1,0,2:T(8,128)(2,1)S(1)} all-gather(bf16[8,32,64]{1,0,2:T(8,128)(2,1)S(1)} %copy.55), channel_id=1, replica_groups=mesh['seq'=8,'res'=4] {'res'}, dimensions={2}, use_global_device_ids=true | all-gather | bytes 163840 | tf_op jit(solution)/shard_map/all_gather | solution.py:174
  150.7 60.2 %while.23 = (s32[]{:T(128)}, f32[4,8,32,256]{3,2,1,0:T(8,128)}, f32[4,8,32,8]{2,3,1,0:T(8,128)S(1)}, bf16[4,8,256,256]{3,2,1,0:T(8,128)(2,1)}, f32[4,8,256]{2,1,...) while((s32[]{:T(128)}, f32[4,8,32,256]{3,2,1,0:T(8,128)}, ...), condition=%wide.region_11.12_spmd, body=%wide.region_8.0_spmd.sunk | while | flops 71366656 | bytes 19509868 | solution.py:52
  150.7 2.7 %constant_dynamic-slice_fusion.5 = (bf16[1,8,256,256]{3,2,1,0:T(8,128)(2,1)S(1)}, bf16[1,8,256,256]{3,2,1,0:T(8,128)(2,1)}) fusion(bf16[4,8,256,256]{3,2,1,0:T(8,128)(2,1)} %get-tuple-element.343, s32[]{:T(128)} %get-tuple-element.328, bf16[4,8,256,256]{3,2,1,0:T(8,128)(2,1)} %get-tuple-element.340), kind=kLoop, calls=%fused_computation.24.clone.1 | loop fusion | bytes 4194308 | tf_op jit(solution)/shard_map/while/body/jit(dynamic_index_in_dim)/dynamic_slice | solution.py:52
  156.0 1.8 fusion.131
  158.5 2.3 %copy.99 = bf16[1,8,256,256]{2,3,1,0:T(8,128)(2,1)} copy(bf16[1,8,256,256]{3,2,1,0:T(8,128)(2,1)} %get-tuple-element.282) | data formatting | bytes 2097152 | tf_op jit(solution)/shard_map/while/body/jit(dynamic_index_in_dim)/dynamic_slice | solution.py:52
  160.8 2.7 %fusion.132 = f32[8,8,32,32]{3,2,1,0:T(8,128)} fusion(bf16[8,256,8,32]{1,3,2,0:T(8,128)(2,1)} %bitcast.153, f32[8,8,32,256]{3,2,1,0:T(8,128)S(1)} %get-tuple-element.284, f32[8,8,32]{2,1,0:T(8,128)S(1)} %get-tuple-element.285), kind=kOutput, calls=%fused_computation.17.clone.1 | convolution fusion | flops 34603008 | bytes 3416064 | tf_op jit(solution)/shard_map/while/body/eval_jaxpr/shij,sjhd->sihd/dot_general | solution.py:74
  163.5 1.5 copy.101
  165.8 2.7 %constant_dynamic-slice_fusion.5 = (bf16[1,8,256,256]{3,2,1,0:T(8,128)(2,1)S(1)}, bf16[1,8,256,256]{3,2,1,0:T(8,128)(2,1)}) fusion(bf16[4,8,256,256]{3,2,1,0:T(8,128)(2,1)} %get-tuple-element.343, s32[]{:T(128)} %get-tuple-element.328, bf16[4,8,256,256]{3,2,1,0:T(8,128)(2,1)} %get-tuple-element.340), kind=kLoop, calls=%fused_computation.24.clone.1 | loop fusion | bytes 4194308 | tf_op jit(solution)/shard_map/while/body/jit(dynamic_index_in_dim)/dynamic_slice | solution.py:52
  171.0 1.8 fusion.131
  173.5 2.3 %copy.99 = bf16[1,8,256,256]{2,3,1,0:T(8,128)(2,1)} copy(bf16[1,8,256,256]{3,2,1,0:T(8,128)(2,1)} %get-tuple-element.282) | data formatting | bytes 2097152 | tf_op jit(solution)/shard_map/while/body/jit(dynamic_index_in_dim)/dynamic_slice | solution.py:52
  175.8 2.7 %fusion.132 = f32[8,8,32,32]{3,2,1,0:T(8,128)} fusion(bf16[8,256,8,32]{1,3,2,0:T(8,128)(2,1)} %bitcast.153, f32[8,8,32,256]{3,2,1,0:T(8,128)S(1)} %get-tuple-element.284, f32[8,8,32]{2,1,0:T(8,128)S(1)} %get-tuple-element.285), kind=kOutput, calls=%fused_computation.17.clone.1 | convolution fusion | flops 34603008 | bytes 3416064 | tf_op jit(solution)/shard_map/while/body/eval_jaxpr/shij,sjhd->sihd/dot_general | solution.py:74
  178.6 1.5 copy.101
  180.8 2.7 %constant_dynamic-slice_fusion.5 = (bf16[1,8,256,256]{3,2,1,0:T(8,128)(2,1)S(1)}, bf16[1,8,256,256]{3,2,1,0:T(8,128)(2,1)}) fusion(bf16[4,8,256,256]{3,2,1,0:T(8,128)(2,1)} %get-tuple-element.343, s32[]{:T(128)} %get-tuple-element.328, bf16[4,8,256,256]{3,2,1,0:T(8,128)(2,1)} %get-tuple-element.340), kind=kLoop, calls=%fused_computation.24.clone.1 | loop fusion | bytes 4194308 | tf_op jit(solution)/shard_map/while/body/jit(dynamic_index_in_dim)/dynamic_slice | solution.py:52
  186.0 1.8 fusion.131
  188.5 2.3 %copy.99 = bf16[1,8,256,256]{2,3,1,0:T(8,128)(2,1)} copy(bf16[1,8,256,256]{3,2,1,0:T(8,128)(2,1)} %get-tuple-element.282) | data formatting | bytes 2097152 | tf_op jit(solution)/shard_map/while/body/jit(dynamic_index_in_dim)/dynamic_slice | solution.py:52
  190.9 2.7 %fusion.132 = f32[8,8,32,32]{3,2,1,0:T(8,128)} fusion(bf16[8,256,8,32]{1,3,2,0:T(8,128)(2,1)} %bitcast.153, f32[8,8,32,256]{3,2,1,0:T(8,128)S(1)} %get-tuple-element.284, f32[8,8,32]{2,1,0:T(8,128)S(1)} %get-tuple-element.285), kind=kOutput, calls=%fused_computation.17.clone.1 | convolution fusion | flops 34603008 | bytes 3416064 | tf_op jit(solution)/shard_map/while/body/eval_jaxpr/shij,sjhd->sihd/dot_general | solution.py:74
  193.6 1.5 copy.101
  195.8 2.7 %constant_dynamic-slice_fusion.5 = (bf16[1,8,256,256]{3,2,1,0:T(8,128)(2,1)S(1)}, bf16[1,8,256,256]{3,2,1,0:T(8,128)(2,1)}) fusion(bf16[4,8,256,256]{3,2,1,0:T(8,128)(2,1)} %get-tuple-element.343, s32[]{:T(128)} %get-tuple-element.328, bf16[4,8,256,256]{3,2,1,0:T(8,128)(2,1)} %get-tuple-element.340), kind=kLoop, calls=%fused_computation.24.clone.1 | loop fusion | bytes 4194308 | tf_op jit(solution)/shard_map/while/body/jit(dynamic_index_in_dim)/dynamic_slice | solution.py:52
  201.1 1.8 fusion.131
  203.6 2.3 %copy.99 = bf16[1,8,256,256]{2,3,1,0:T(8,128)(2,1)} copy(bf16[1,8,256,256]{3,2,1,0:T(8,128)(2,1)} %get-tuple-element.282) | data formatting | bytes 2097152 | tf_op jit(solution)/shard_map/while/body/jit(dynamic_index_in_dim)/dynamic_slice | solution.py:52
  205.9 2.7 %fusion.132 = f32[8,8,32,32]{3,2,1,0:T(8,128)} fusion(bf16[8,256,8,32]{1,3,2,0:T(8,128)(2,1)} %bitcast.153, f32[8,8,32,256]{3,2,1,0:T(8,128)S(1)} %get-tuple-element.284, f32[8,8,32]{2,1,0:T(8,128)S(1)} %get-tuple-element.285), kind=kOutput, calls=%fused_computation.17.clone.1 | convolution fusion | flops 34603008 | bytes 3416064 | tf_op jit(solution)/shard_map/while/body/eval_jaxpr/shij,sjhd->sihd/dot_general | solution.py:74
  208.6 1.5 copy.101
  211.1 2.6 %div.59 = f32[32,32,8,32]{3,2,1,0:T(8,128)} broadcast(f32[32,32,8]{2,1,0:T(8,128)S(1)} %copy.60), dimensions={0,1,2} | broadcast | bytes 1081344 | tf_op jit(solution)/shard_map/div | solution.py:188
  213.7 3.4 %div.60 = f32[32,32,256]{2,1,0:T(8,128)S(1)} reshape(f32[32,32,8,32]{3,2,1,0:T(8,128)} %div.59) | data formatting | bytes 2097152 | tf_op jit(solution)/shard_map/div | solution.py:188
  218.3 2.0 fusion.97
  220.8 2.4 %fusion.39 = f32[32,32,256]{2,1,0:T(8,128)} fusion(f32[32,32,256]{2,1,0:T(8,128)S(1)} %get-tuple-element.179, bf16[1024,256]{1,0:T(8,128)(2,1)S(1)} %copy-done, bf16[256,1024]{1,0:T(8,128)(2,1)S(1)} %copy-done.15, f32[256]{0:T(256)S(1)} %copy-done.26, f32[32,32]{1,0:T(8,128)S(1)} %add_rsqrt_fusion.1, f32[32,32]{1,0:T(8,128)S(1)} %broadcast_multiply_fusion.4), kind=kOutput, calls=%fused_computation.54 | convolution fusion | flops 1077149696 | bytes 3154944 | tf_op jit(solution)/shard_map/dot_general | solution.py:30
  (139 shorter events, 35.6 us)
Async XLA Ops:
  7.2 213.6 %copy-start = (bf16[1024,256]{1,0:T(8,128)(2,1)S(1)}, bf16[1024,256]{1,0:T(8,128)(2,1)}, u32[]{:S(2)}) copy-start(bf16[1024,256]{1,0:T(8,128)(2,1)} %param.41) | copy-start | bytes 1572868
  7.2 50.3 %copy-start.4 = (bf16[32,32,256]{2,1,0:T(8,128)(2,1)S(1)}, bf16[32,32,256]{2,1,0:T(8,128)(2,1)}, u32[]{:S(2)}) copy-start(bf16[32,32,256]{2,1,0:T(8,128)(2,1)} %param.23) | copy-start | bytes 1572868
  7.2 50.3 %copy-start.23 = (f32[256]{0:T(256)S(1)}, f32[256]{0:T(256)}, u32[]{:S(2)}) copy-start(f32[256]{0:T(256)} %param.33) | copy-start | bytes 3076
  7.2 50.3 %copy-start.17 = (bf16[256,256]{1,0:T(8,128)(2,1)S(1)}, bf16[256,256]{1,0:T(8,128)(2,1)}, u32[]{:S(2)}) copy-start(bf16[256,256]{1,0:T(8,128)(2,1)} %param.34) | copy-start | bytes 393220
  7.2 78.9 %all-gather.3.cloned.1.call-start = ((), (), s32[]{:S(2)}) async-start(), calls=%async_computation.2 | async-start | bytes 4718592 | tf_op jit(solution)/shard_map/all_gather | solution.py:128
  42.5 27.9 %all-to-all-start.1 = ((bf16[4,2,1024]{2,1,0:T(2,128)(2,1)}), bf16[4,2,1024]{2,1,0:T(2,128)(2,1)S(1)}, u32[]{:S(2)}, u32[]{:S(2)}) async-start(bf16[4,2,1024]{2,1,0:T(2,128)(2,1)} %reshape.217), calls=%async_computation.1 | async-start | bytes 32768 | tf_op jit(solution)/shard_map/all_to_all | solution.py:139
  55.1 2.3 %copy-start.11 = (f32[32,32]{1,0:T(8,128)}, f32[32,32]{1,0:T(8,128)S(1)}, u32[]{:S(2)}) copy-start(f32[32,32]{1,0:T(8,128)S(1)} %add_rsqrt_fusion.3) | copy-start | bytes 12292
  70.5 22.2 %copy-start.21 = (bf16[256,32]{0,1:T(8,128)(2,1)S(1)}, bf16[256,32]{0,1:T(8,128)(2,1)}, u32[]{:S(2)}) copy-start(bf16[256,32]{0,1:T(8,128)(2,1)} %param.29) | copy-start | bytes 49156
  70.5 22.2 %copy-start.22 = (f32[256]{0:T(256)S(1)}, f32[256]{0:T(256)}, u32[]{:S(2)}) copy-start(f32[256]{0:T(256)} %param.27) | copy-start | bytes 3076
  86.1 3.5 %copy-start.1 = (bf16[32,256,256]{2,1,0:T(8,128)(2,1)S(1)}, bf16[32,256,256]{2,1,0:T(8,128)(2,1)}, u32[]{:S(2)}) copy-start(bf16[32,256,256]{2,1,0:T(8,128)(2,1)} %all-gather.3.cloned.1.call-done) | copy-start | bytes 12582916
  92.1 0.6 copy-start.9
  102.4 13.8 %all-to-all-start = ((bf16[4,2,32768]{2,1,0:T(2,128)(2,1)}), bf16[4,2,32768]{2,1,0:T(2,128)(2,1)S(1)}, u32[]{:S(2)}, u32[]{:S(2)}) async-start(bf16[4,2,32768]{2,1,0:T(2,128)(2,1)} %reshape.215), calls=%async_computation | async-start | bytes 1048576 | tf_op jit(solution)/shard_map/all_to_all | solution.py:138
  106.1 5.8 %copy-start.2 = (bf16[32,256,256]{2,1,0:T(8,128)(2,1)S(1)}, bf16[32,256,256]{2,1,0:T(8,128)(2,1)}, u32[]{:S(2)}) copy-start(bf16[32,256,256]{2,1,0:T(8,128)(2,1)} %all-gather.3.cloned.1.call-done) | copy-start | bytes 12582916
  106.1 5.8 %copy-start.10 = (f32[32,256]{1,0:T(8,128)S(1)}, f32[32,256]{1,0:T(8,128)}, u32[]{:S(2)}) copy-start(f32[32,256]{1,0:T(8,128)} %copy-done.9) | copy-start | bytes 98308
  106.1 5.8 %copy-start.18 = (bf16[256,256]{1,0:T(8,128)(2,1)S(1)}, bf16[256,256]{1,0:T(8,128)(2,1)}, u32[]{:S(2)}) copy-start(bf16[256,256]{1,0:T(8,128)(2,1)} %param.35) | copy-start | bytes 393220
  106.1 5.8 %copy-start.24 = (f32[256]{0:T(256)S(1)}, f32[256]{0:T(256)}, u32[]{:S(2)}) copy-start(f32[256]{0:T(256)} %param.33) | copy-start | bytes 3076
  117.3 6.0 %copy-start.16 = (bf16[1024,128]{1,0:T(8,128)(2,1)S(1)}, bf16[1024,128]{1,0:T(8,128)(2,1)}, u32[]{:S(2)}) copy-start(bf16[1024,128]{1,0:T(8,128)(2,1)} %param.30) | copy-start | bytes 786436
  117.3 6.0 %copy-start.27 = (s32[2]{0:T(128)S(1)}, s32[2]{0:T(128)}, u32[]{:S(2)}) copy-start(s32[2]{0:T(128)} %iota_multiply_fusion) | copy-start | bytes 28
  123.3 15.9 %copy-start.6 = (f32[32,64,128]{2,1,0:T(8,128)S(1)}, f32[32,64,128]{2,1,0:T(8,128)}, u32[]{:S(2)}) copy-start(f32[32,64,128]{2,1,0:T(8,128)} %param.26) | copy-start | bytes 3145732
  139.2 2.6 %copy-start.13 = (bf16[128,8]{0,1:T(8,128)(2,1)S(1)}, bf16[128,8]{0,1:T(8,128)(2,1)}, u32[]{:S(2)}) copy-start(bf16[128,8]{0,1:T(8,128)(2,1)} %param.32) | copy-start | bytes 6148
  139.2 2.6 %copy-start.14 = (f32[128]{0:T(128)S(1)}, f32[128]{0:T(128)}, u32[]{:S(2)}) copy-start(f32[128]{0:T(128)} %param.31) | copy-start | bytes 1540
  139.2 11.5 %copy-start.8 = (f32[4,8,32,8]{2,3,1,0:T(8,128)S(1)}, f32[4,8,32,8]{2,3,1,0:T(8,128)}, u32[]{:S(2)}) copy-start(f32[4,8,32,8]{2,3,1,0:T(8,128)} %custom-call.2) | copy-start | bytes 98308
  140.9 1.0 copy-start.3
  211.1 6.0 %copy-start.7 = (f32[4,8,32,256]{3,2,1,0:T(8,128)S(1)}, f32[4,8,32,256]{3,2,1,0:T(8,128)}, u32[]{:S(2)}) copy-start(f32[4,8,32,256]{3,2,1,0:T(8,128)} %get-tuple-element.88) | copy-start | bytes 3145732
  213.7 4.6 %copy-start.5 = (bf16[32,32,256]{2,1,0:T(8,128)(2,1)S(1)}, bf16[32,32,256]{2,1,0:T(8,128)(2,1)}, u32[]{:S(2)}) copy-start(bf16[32,32,256]{2,1,0:T(8,128)(2,1)} %param.23) | copy-start | bytes 1572868
  213.7 4.6 %copy-start.12 = (f32[32,32]{1,0:T(8,128)S(1)}, f32[32,32]{1,0:T(8,128)}, u32[]{:S(2)}) copy-start(f32[32,32]{1,0:T(8,128)} %copy-done.11) | copy-start | bytes 12292
  213.7 4.6 %copy-start.19 = (bf16[256,256]{1,0:T(8,128)(2,1)S(1)}, bf16[256,256]{1,0:T(8,128)(2,1)}, u32[]{:S(2)}) copy-start(bf16[256,256]{1,0:T(8,128)(2,1)} %param.38) | copy-start | bytes 393220
  213.7 4.6 %copy-start.20 = (bf16[256,256]{1,0:T(8,128)(2,1)S(1)}, bf16[256,256]{1,0:T(8,128)(2,1)}, u32[]{:S(2)}) copy-start(bf16[256,256]{1,0:T(8,128)(2,1)} %param.37) | copy-start | bytes 393220
  213.7 4.6 %copy-start.25 = (f32[256]{0:T(256)S(1)}, f32[256]{0:T(256)}, u32[]{:S(2)}) copy-start(f32[256]{0:T(256)} %param.33) | copy-start | bytes 3076
  218.3 2.4 %copy-start.15 = (bf16[256,1024]{1,0:T(8,128)(2,1)S(1)}, bf16[256,1024]{1,0:T(8,128)(2,1)}, u32[]{:S(2)}) copy-start(bf16[256,1024]{1,0:T(8,128)(2,1)} %param.40) | copy-start | bytes 1572868
  218.3 2.4 %copy-start.26 = (f32[256]{0:T(256)S(1)}, f32[256]{0:T(256)}, u32[]{:S(2)}) copy-start(f32[256]{0:T(256)} %param.39) | copy-start | bytes 3076
Sparse Core Ops, SparseCore 0:
  10.2 75.8 all-gather.2
